TPU v7x, 32 devices: a whole 2x2x4 slice. The times are simulated.
32 devices in a mesh: feat: 8 (over z, y), samp: 4 (over x, core).
Axes of the slice: x: 2, y: 2, z: 4, core: 2. Of those that a mesh axis runs over, the one named last changes fastest.
Arguments:
- design: bfloat16 [14336, 8192], P('samp', 'feat'), may hold values from -0.0625 to 0.0625
- targets: bfloat16 [14336, 128], P('samp'), may hold values from -26 to 26
- warm_start: float32 [8192, 128], P('feat'), may hold values from -0.6 to 0.6
- active_mask: int32 [2, 8192], P(None, 'feat'), may hold values 0 or 1
- penalty_index: int32 [1], replicated, may hold values from 0 to 7
Outputs:
- coefficients: float32 [8192, 128], P('feat')
- correlations: float32 [3, 8192], P(None, 'feat')
- relative_gaps: float32 [3], replicated
- pruned_counts: float32 [2], replicated
All inputs are finite; a program needn't handle non-finite values. No bound on the sum of `active_mask` on one device may be relied on, other than what follows from the above.
Results may differ from a plain program's by a relative error of at most 0.0024.
The roundings to bfloat16 on the way count: a program that leaves them out, or rounds other values in their place, can miss the bound.
Values may be sent and summed in bfloat16 or wider, within the bound.
A program may use at most 64 MiB of HBM per device.

v0:
```python
import jax
import jax.numpy as jnp
from jax import lax
from jax.sharding import PartitionSpec as P

ITERS = 2


def group_norms(matrix):
    return jnp.sqrt(jnp.sum(matrix * matrix, axis=1))


def transpose_product(design, right_side):
    return lax.dot_general(
        design, right_side, (((0,), (0,)), ((), ())), preferred_element_type=jnp.float32
    )


def local(design, targets, warm_start, active_mask, penalty_index):
    row_count, col_count = design.shape
    feat_size = lax.axis_size("feat")
    feat_slot = lax.axis_index("feat")
    block_rows = row_count // feat_size
    samp_first = (lax.axis_index("samp") == 0).astype(jnp.float32)
    corr_local = transpose_product(design, targets)
    squares_local = jnp.sum(jnp.square(design.astype(jnp.float32)), axis=0)
    corr_y, column_squares = lax.psum((corr_local, squares_local), "samp")
    penalty_max = lax.pmax(jnp.max(group_norms(corr_y)), "feat")
    penalty = penalty_max / (8.0 + 4.0 * penalty_index[0].astype(jnp.float32))
    step_sizes = 0.5 / (1.0 + column_squares)
    current = warm_start
    correlations = []
    relative_gaps = []
    pruned_counts = []
    own_targets = lax.dynamic_slice_in_dim(targets, feat_slot * block_rows, block_rows, 0)
    for iteration in range(ITERS + 1):
        current_half = current.astype(jnp.bfloat16)
        fitted_part = jnp.dot(design, current_half, preferred_element_type=jnp.float32)
        fitted = lax.psum(fitted_part, "feat")
        residual_all = (targets.astype(jnp.float32) - fitted).astype(jnp.bfloat16)
        residual = lax.dynamic_slice_in_dim(residual_all, feat_slot * block_rows, block_rows, 0)
        grad_local = transpose_product(design, residual_all)
        resid_float = residual.astype(jnp.float32)
        rr_local = jnp.sum(resid_float * resid_float)
        ry_local = jnp.sum(resid_float * own_targets.astype(jnp.float32))
        bn_local = samp_first * jnp.sum(group_norms(current))
        if iteration < ITERS:
            keep = active_mask[iteration].astype(jnp.float32)
            pruned_local = samp_first * jnp.sum(1.0 - keep)
        else:
            pruned_local = jnp.zeros((), jnp.float32)
        gradient = lax.psum(grad_local, "samp")
        grad_norms = group_norms(gradient)
        local_max = jnp.max(grad_norms)
        grad_top = lax.pmax(local_max, "feat")
        rr_sum, ry_sum, bn_sum, pruned_sum = lax.psum(
            (rr_local, ry_local, bn_local, pruned_local), ("feat", "samp")
        )
        scale = jnp.maximum(penalty, grad_top)
        correlations.append(grad_norms / scale)
        primal = 0.5 * rr_sum + penalty * bn_sum
        ratio = penalty / scale
        dual = ratio * ry_sum - 0.5 * ratio * ratio * rr_sum
        relative_gaps.append((primal - dual) / (primal + 1.0))
        if iteration < ITERS:
            pruned_counts.append(pruned_sum)
            moved = current + step_sizes[:, None] * gradient
            moved_norms = group_norms(moved)
            cutoff = step_sizes * penalty
            factor = jnp.maximum(moved_norms - cutoff, 0.0) / jnp.maximum(moved_norms, cutoff)
            current = (keep * factor)[:, None] * moved
    return (current, jnp.stack(correlations), jnp.stack(relative_gaps), jnp.stack(pruned_counts))


def solution(mesh):
    placed = (P("samp", "feat"), P("samp", None), P("feat", None), P(None, "feat"), P())
    return jax.shard_map(
        local,
        mesh=mesh,
        in_specs=placed,
        out_specs=(P("feat", None), P(None, "feat"), P(), P()),
        check_vma=False,
    )
```

profile of v0, /device:TPU:0, one launch (start us, length us, event | category | flops | bytes accessed | tf_op | source)
XLA Modules:
  0.0 527.3 jit_solution(8647449387170644454)
XLA Ops:
  7.2 6.5 %fusion.5 = f32[3584,128]{1,0:T(8,128)} fusion(bf16[3584,1024]{1,0:T(8,128)(2,1)} %param.5, f32[1024,128]{1,0:T(8,128)} %param.7), kind=kOutput, calls=%fused_computation.33 | convolution fusion | flops 939655168 | bytes 9699328 | tf_op jit(solution)/shard_map/dot_general | solution.py:38
  13.7 0.0 all-reduce.20.cloned.1.call-start
  13.8 6.0 %fusion.13 = f32[1024,128]{1,0:T(8,128)} fusion(bf16[3584,1024]{1,0:T(8,128)(2,1)} %param.5, bf16[3584,128]{1,0:T(8,128)(2,1)S(1)} %copy-done), kind=kOutput, calls=%fused_computation.61 | convolution fusion | flops 939524096 | bytes 8781824 | tf_op jit(solution)/shard_map/dot_general | solution.py:14
  19.8 92.7 %all-reduce.10.cloned.1.call-done = f32[3584,128]{1,0:T(8,128)} async-done(((f32[3584,128]{1,0:T(8,128)}), f32[3584,128]{1,0:T(8,128)}) %all-reduce.10.cloned.1.call-update) | async-done | bytes 1835024 | tf_op jit(solution)/shard_map/psum | solution.py:39
  112.5 1.7 fusion
  114.1 5.0 convolution_bitcast_fusion.4
  119.2 0.0 all-reduce.12.cloned.1.call-start
  119.3 4.6 multiply_reduce_fusion
  123.9 1.0 copy.9
  125.5 7.1 %psum.133 = f32[1024]{0:T(1024)S(1)} all-reduce(f32[1024]{0:T(1024)S(1)} %multiply_reduce_fusion), channel_id=1, replica_groups=mesh['feat'=8,'samp'=4] {'samp'}, use_global_device_ids=true, to_apply=%region_1.0 | all-reduce | flops 1024 | bytes 8192 | tf_op jit(solution)/shard_map/psum | solution.py:27
  132.7 22.5 %all-reduce.20.cloned.1.call-done = (f32[1024,128]{0,1:T(8,128)}, f32[1024,128]{1,0:T(8,128)}) async-done(((f32[1024,128]{0,1:T(8,128)}, f32[1024,128]{1,0:T(8,128)}), (f32[1024,128]{0,1:T(8,128)}, f32[1024,128]{1,0:T(8,128)})) %all-reduce.20.cloned.1.call-update) | async-done | bytes 1048592 | tf_op jit(solution)/shard_map/psum | solution.py:52
  155.2 1.2 multiply_reduce_fusion.8
  156.5 0.6 sqrt_reduce_fusion.3
  157.1 22.0 %pmax.28 = f32[]{:T(128)} all-reduce(f32[]{:T(128)} %sqrt_reduce_fusion.3), channel_id=1, replica_groups=mesh['feat'=8,'samp'=4] {'feat'}, use_global_device_ids=true, to_apply=%region_8.0 | all-reduce | flops 1 | bytes 8 | tf_op jit(solution)/shard_map/pmax | solution.py:28
  179.7 1.3 multiply_reduce_fusion.9
  181.1 0.6 subtract_reduce_fusion.1
  181.7 6.4 %convolution_bitcast_fusion.1 = f32[3584,128]{1,0:T(8,128)} fusion(bf16[3584,1024]{1,0:T(8,128)(2,1)} %param.5, f32[1024,128]{0,1:T(8,128)S(1)} %get-tuple-element.36, f32[1024]{0:T(1024)S(1)} %get-tuple-element.41), kind=kOutput, calls=%fused_computation.2 | convolution fusion | flops 939786240 | bytes 9703424 | tf_op jit(solution)/shard_map/dot_general | solution.py:38
  188.1 0.0 all-reduce.14.cloned.1.call-start
  188.1 92.7 %all-reduce.12.cloned.1.call-done = f32[3584,128]{1,0:T(8,128)} async-done(((f32[3584,128]{1,0:T(8,128)}), f32[3584,128]{1,0:T(8,128)}) %all-reduce.12.cloned.1.call-update) | async-done | bytes 1835024 | tf_op jit(solution)/shard_map/psum | solution.py:39
  280.9 1.7 fusion.1
  282.6 5.0 convolution_bitcast_fusion.3
  287.6 0.2 all-reduce.16.cloned.1.call-start
  287.8 32.8 %all-reduce.14.cloned.1.call-done = f32[1024,128]{0,1:T(8,128)} async-done(((f32[1024,128]{0,1:T(8,128)}), f32[1024,128]{0,1:T(8,128)}) %all-reduce.14.cloned.1.call-update) | async-done | bytes 524304 | tf_op jit(solution)/shard_map/psum | solution.py:52
  320.7 1.2 multiply_reduce_fusion.2
  321.9 0.7 subtract_reduce_fusion
  322.6 1.2 multiply_reduce_fusion.1
  323.8 0.8 copy-done.2
  324.5 6.4 %convolution_bitcast_fusion = f32[3584,128]{1,0:T(8,128)} fusion(bf16[3584,1024]{1,0:T(8,128)(2,1)} %param.5, f32[1024,128]{0,1:T(8,128)S(1)} %get-tuple-element.34), kind=kOutput, calls=%fused_computation.1 | convolution fusion | flops 939655168 | bytes 9699328 | tf_op jit(solution)/shard_map/dot_general | solution.py:38
  331.0 0.0 all-reduce.18.cloned.1.call-start
  331.0 0.2 multiply_reduce_fusion.3
  331.2 0.6 sqrt_reduce_fusion.2
  333.1 0.6 sqrt_reduce_fusion.6
  333.7 0.6 sqrt_reduce_fusion.1
  334.3 92.8 %all-reduce.16.cloned.1.call-done = f32[3584,128]{1,0:T(8,128)} async-done(((f32[3584,128]{1,0:T(8,128)}), f32[3584,128]{1,0:T(8,128)}) %all-reduce.16.cloned.1.call-update) | async-done | bytes 1835024 | tf_op jit(solution)/shard_map/psum | solution.py:39
  427.1 1.7 fusion.2
  428.7 0.9 copy-done.1
  429.7 5.1 convolution_bitcast_fusion.2
  434.8 0.6 sqrt_reduce_fusion
  435.4 1.0 copy.12
  438.3 0.6 sqrt_reduce_fusion.5
  439.0 1.7 fusion.10
  440.7 41.8 %all-reduce = (f32[]{:T(128)}, f32[]{:T(128)}, f32[]{:T(128)}, f32[]{:T(128)}, f32[]{:T(128)}, /*index=5*/f32[]{:T(128)}, f32[]{:T(128)}, f32[]{:T(128)}, f32[]{:T(128)}, f32[1]{0:T(128)}, /*index=10*/f32[1]{0:T(128)}) all-reduce(f32[]{:T(128)} %get-tuple-element.12, ...), channel_id=1, replica_groups=mesh['feat'=8,'samp'=4] {'feat','samp'}, use_global_device_ids=true, to_apply=%region_38.0 | all-reduce | flops 11 | bytes 88 | tf_op jit(solution)/shard_map/psum | solution.py:56
  486.2 1.9 pad_maximum_fusion.2
  488.1 1.1 multiply_reduce_fusion.4
  489.2 0.7 sqrt_reduce_fusion.4
  489.9 21.7 %all-reduce.1 = (f32[]{:T(128)}, f32[]{:T(128)}, f32[]{:T(128)}) all-reduce(f32[]{:T(128)} %sqrt_reduce_fusion.4, f32[]{:T(128)} %sqrt_reduce_fusion.5, f32[]{:T(128)} %sqrt_reduce_fusion.6), channel_id=1, replica_groups=mesh['feat'=8,'samp'=4] {'feat'}, use_global_device_ids=true, to_apply=%region_22.0 | all-reduce | flops 3 | bytes 24 | tf_op jit(solution)/shard_map/pmax | solution.py:55
  519.2 0.6 pad_maximum_fusion.1
  519.8 0.6 pad_maximum_fusion
  (25 shorter events, 0.2 us)
Async XLA Ops:
  7.2 6.6 %copy-start = (bf16[3584,128]{1,0:T(8,128)(2,1)S(1)}, bf16[3584,128]{1,0:T(8,128)(2,1)}, u32[]{:S(2)}) copy-start(bf16[3584,128]{1,0:T(8,128)(2,1)} %param.6) | copy-start | bytes 2752516
  7.2 105.3 %all-reduce.10.cloned.1.call-start = ((), (), s32[]{:S(2)}) async-start(), calls=%async_computation | async-start | bytes 3670016 | tf_op jit(solution)/shard_map/psum | solution.py:39
  13.7 141.5 %all-reduce.20.cloned.1.call-start = ((), (), s32[]{:S(2)}) async-start(), calls=%async_computation.5 | async-start | bytes 2097152 | tf_op jit(solution)/shard_map/psum | solution.py:52
  119.2 4.7 copy-start.4
  119.2 13.5 %copy-start.6 = (s32[2,1024]{1,0:T(2,128)S(1)}, s32[2,1024]{1,0:T(2,128)}, u32[]{:S(2)}) copy-start(s32[2,1024]{1,0:T(2,128)} %param.8) | copy-start | bytes 24580
  119.2 161.7 %all-reduce.12.cloned.1.call-start = ((), (), s32[]{:S(2)}) async-start(), calls=%async_computation.1 | async-start | bytes 3670016 | tf_op jit(solution)/shard_map/psum | solution.py:39
  188.1 132.6 %all-reduce.14.cloned.1.call-start = ((), (), s32[]{:S(2)}) async-start(), calls=%async_computation.2 | async-start | bytes 1048576 | tf_op jit(solution)/shard_map/psum | solution.py:52
  287.6 139.5 %all-reduce.16.cloned.1.call-start = ((), (), s32[]{:S(2)}) async-start(), calls=%async_computation.3 | async-start | bytes 3670016 | tf_op jit(solution)/shard_map/psum | solution.py:39
  323.7 0.8 copy-start.2
  323.8 7.3 %copy-start.5 = (f32[1024,128]{1,0:T(8,128)S(1)}, f32[1024,128]{1,0:T(8,128)}, u32[]{:S(2)}) copy-start(f32[1024,128]{1,0:T(8,128)} %param.7) | copy-start | bytes 1572868
  331.0 157.1 %all-reduce.18.cloned.1.call-start = ((), (), s32[]{:S(2)}) async-start(), calls=%async_computation.4 | async-start | bytes 1048576 | tf_op jit(solution)/shard_map/psum | solution.py:52
  428.7 0.9 copy-start.1
  429.7 5.8 %copy-start.3 = (f32[1024,128]{0,1:T(8,128)S(1)}, f32[1024,128]{0,1:T(8,128)}, u32[]{:S(2)}) copy-start(f32[1024,128]{0,1:T(8,128)} %copy-done.2) | copy-start | bytes 1572868
Sparse Core Ops, SparseCore 0:
  13.9 98.5 all-reduce.9
  119.3 35.8 all-reduce.19
  188.2 92.6 all-reduce.11
  287.7 32.9 all-reduce.13
  331.1 95.9 all-reduce.15
  434.9 33.1 all-reduce.17
where the time goes:
time: 528 us; the launch traced here: 527 us
  waiting for transfers between devices  334 us (63%)
  blocking collectives  92.5 us (18%)
  matrix products  40.5 us (8%)
  between operations  30.1 us (6%)
  other arithmetic  26.4 us (5%)
    psum x3, waiting for transfers between devices, local(): fitted = lax.psum(fitted_part, 'feat')  278 us
    psum x3, waiting for transfers between devices, local(): gradient = lax.psum(grad_local, 'samp')  55.4 us
    psum x1, blocking collectives, local(): lax.psum((rr_local, ry_local, bn_local, pruned_local), ('feat', 'samp'))  41.8 us
    pmax x1, blocking collectives, local(): penalty_max = lax.pmax(jnp.max(group_norms(corr_y)), 'feat')  22 us
    pmax x1, blocking collectives, local(): grad_top = lax.pmax(local_max, 'feat')  21.7 us
    dot_general x4, matrix products, transpose_product(): lax.dot_general(design, right_side, (((0,), (0,)), ((), ())), preferred_e...  21.2 us
    dot_general x3, matrix products, local(): jnp.dot(design, current_half, preferred_element_type=jnp.float32)  19.3 us
  transfers between devices with their start and end apart: 6, of which 5 were waited for; matrix products, arithmetic and copies ran while one was open for 4% of the time, Pallas kernels for 0%

commit v1 on v0

--- a/solution.py
+++ b/solution.py
@@ -36,7 +36,11 @@
     for iteration in range(ITERS + 1):
         current_half = current.astype(jnp.bfloat16)
         fitted_part = jnp.dot(design, current_half, preferred_element_type=jnp.float32)
-        fitted = lax.psum(fitted_part, "feat")
+        size = lax.axis_size("feat")
+        fitted, far = (fitted_part, 1)
+        while far < size:
+            fitted = fitted + lax.ppermute(fitted, "feat", [(i, i ^ far) for i in range(size)])
+            far = 2 * far
         residual_all = (targets.astype(jnp.float32) - fitted).astype(jnp.bfloat16)
         residual = lax.dynamic_slice_in_dim(residual_all, feat_slot * block_rows, block_rows, 0)
         grad_local = transpose_product(design, residual_all)

time: 528 us -> 706 us (1.34)
  waiting for transfers between devices: 334 us -> 512 us
  starting transfers between devices: 0.43 us -> 13.8 us
  matrix products: 40.5 us -> 28 us
    ppermute x0 -> x9, waiting for transfers between devices: none -> 455 us  [local(): lax.ppermute(fitted, 'feat', [(i, i ^ far) for i in range(size)])]
    psum x3 -> x0, waiting for transfers between devices: 278 us -> none  [local(): fitted = lax.psum(fitted_part, 'feat')]
    ppermute x0 -> x9, starting transfers between devices: none -> 13.7 us  [local(): lax.ppermute(fitted, 'feat', [(i, i ^ far) for i in range(size)])]
    dot_general x4, matrix products: 21.2 us -> 12 us  [transpose_product(): lax.dot_general(design, right_side, (((0,), (0,)), ((), ())), preferred_e...]
  transfers between devices with their start and end apart: 6 -> 12, of which waited for: 5 -> 11; matrix products, arithmetic and copies ran while one was open for 4% -> 2% of each run, Pallas kernels for 0% -> 0%
where the time goes in v1:
time: 706 us; the launch traced here: 705 us
  waiting for transfers between devices  512 us (73%)
  blocking collectives  91.6 us (13%)
  between operations  29.8 us (4%)
  matrix products  28 us (4%)
  other arithmetic  26.7 us (4%)
  starting transfers between devices  13.8 us (2%)
    ppermute x9, waiting for transfers between devices, local(): lax.ppermute(fitted, 'feat', [(i, i ^ far) for i in range(size)])  455 us
    psum x3, waiting for transfers between devices, local(): gradient = lax.psum(grad_local, 'samp')  56.2 us
    psum x1, blocking collectives, local(): lax.psum((rr_local, ry_local, bn_local, pruned_local), ('feat', 'samp'))  41.7 us
    pmax x1, blocking collectives, local(): penalty_max = lax.pmax(jnp.max(group_norms(corr_y)), 'feat')  22.2 us
    pmax x1, blocking collectives, local(): grad_top = lax.pmax(local_max, 'feat')  21.3 us
    dot_general x3, matrix products, local(): jnp.dot(design, current_half, preferred_element_type=jnp.float32)  16 us
  transfers between devices with their start and end apart: 12, of which 11 were waited for; matrix products, arithmetic and copies ran while one was open for 2% of the time, Pallas kernels for 0%

profile of v1, /device:TPU:0, one launch (start us, length us, event | category | flops | bytes accessed | tf_op | source)
XLA Modules:
  0.0 704.7 jit_solution(10835733695531140306)
XLA Ops:
  7.2 5.4 fusion.5
  12.6 3.1 collective-permute-start
  15.7 40.0 %collective-permute-done = f32[3584,128]{1,0:T(8,128)S(1)} collective-permute-done((f32[3584,128]{1,0:T(8,128)S(1)}, f32[3584,128]{1,0:T(8,128)S(1)}, u32[]{:S(2)}, u32[]{:S(2)}) %collective-permute-start) | collective-permute-done | bytes 1835040 | tf_op jit(solution)/shard_map/ppermute | solution.py:42
  55.9 1.9 collective-permute-start.1
  57.8 39.4 %collective-permute-done.1 = f32[3584,128]{1,0:T(8,128)S(1)} collective-permute-done((f32[3584,128]{1,0:T(8,128)S(1)}, f32[3584,128]{1,0:T(8,128)S(1)}, u32[]{:S(2)}, u32[]{:S(2)}) %collective-permute-start.1) | collective-permute-done | bytes 1835040 | tf_op jit(solution)/shard_map/ppermute | solution.py:42
  97.4 2.6 collective-permute-start.2
  100.0 2.9 fusion.13
  102.9 75.1 %collective-permute-done.2 = f32[3584,128]{1,0:T(8,128)S(1)} collective-permute-done((f32[3584,128]{1,0:T(8,128)S(1)}, f32[3584,128]{1,0:T(8,128)S(1)}, u32[]{:S(2)}, u32[]{:S(2)}) %collective-permute-start.2) | collective-permute-done | bytes 1835040 | tf_op jit(solution)/shard_map/ppermute | solution.py:42
  178.3 2.0 convolution_bitcast_fusion.4
  180.4 4.6 multiply_reduce_fusion
  185.0 1.0 copy.9
  186.7 6.4 psum.112
  193.1 24.5 %all-reduce.11.cloned.1.call-done = (f32[1024,128]{0,1:T(8,128)}, f32[1024,128]{1,0:T(8,128)}) async-done(((f32[1024,128]{0,1:T(8,128)}, f32[1024,128]{1,0:T(8,128)}), (f32[1024,128]{0,1:T(8,128)}, f32[1024,128]{1,0:T(8,128)})) %all-reduce.11.cloned.1.call-update) | async-done | bytes 1048592 | tf_op jit(solution)/shard_map/psum | solution.py:56
  217.7 1.2 multiply_reduce_fusion.8
  218.9 0.6 sqrt_reduce_fusion.3
  219.5 22.2 %pmax.28 = f32[]{:T(128)} all-reduce(f32[]{:T(128)} %sqrt_reduce_fusion.3), channel_id=1, replica_groups=mesh['feat'=8,'samp'=4] {'feat'}, use_global_device_ids=true, to_apply=%region_7.0 | all-reduce | flops 1 | bytes 8 | tf_op jit(solution)/shard_map/pmax | solution.py:28
  242.3 1.3 multiply_reduce_fusion.9
  244.3 5.2 convolution_bitcast_fusion.1
  249.6 37.4 %collective-permute-done.3 = f32[3584,128]{1,0:T(8,128)S(1)} collective-permute-done((f32[3584,128]{1,0:T(8,128)S(1)}, f32[3584,128]{1,0:T(8,128)S(1)}, u32[]{:S(2)}, u32[]{:S(2)}) %collective-permute-start.3) | collective-permute-done | bytes 1835040 | tf_op jit(solution)/shard_map/ppermute | solution.py:42
  287.3 37.7 %collective-permute-done.4 = f32[3584,128]{1,0:T(8,128)S(1)} collective-permute-done((f32[3584,128]{1,0:T(8,128)S(1)}, f32[3584,128]{1,0:T(8,128)S(1)}, u32[]{:S(2)}, u32[]{:S(2)}) %collective-permute-start.4) | collective-permute-done | bytes 1835040 | tf_op jit(solution)/shard_map/ppermute | solution.py:42
  325.3 74.8 %collective-permute-done.5 = f32[3584,128]{1,0:T(8,128)S(1)} collective-permute-done((f32[3584,128]{1,0:T(8,128)S(1)}, f32[3584,128]{1,0:T(8,128)S(1)}, u32[]{:S(2)}, u32[]{:S(2)}) %collective-permute-start.5) | collective-permute-done | bytes 1835040 | tf_op jit(solution)/shard_map/ppermute | solution.py:42
  400.4 2.0 convolution_bitcast_fusion.3
  402.5 31.7 %all-reduce.7.cloned.1.call-done = f32[1024,128]{0,1:T(8,128)} async-done(((f32[1024,128]{0,1:T(8,128)}), f32[1024,128]{0,1:T(8,128)}) %all-reduce.7.cloned.1.call-update) | async-done | bytes 524304 | tf_op jit(solution)/shard_map/psum | solution.py:56
  434.1 1.2 multiply_reduce_fusion.2
  435.4 0.7 subtract_reduce_fusion
  436.0 1.2 multiply_reduce_fusion.1
  437.2 5.4 convolution_bitcast_fusion
  442.6 1.5 collective-permute-start.6
  444.2 39.1 %collective-permute-done.6 = f32[3584,128]{1,0:T(8,128)S(1)} collective-permute-done((f32[3584,128]{1,0:T(8,128)S(1)}, f32[3584,128]{1,0:T(8,128)S(1)}, u32[]{:S(2)}, u32[]{:S(2)}) %collective-permute-start.6) | collective-permute-done | bytes 1835040 | tf_op jit(solution)/shard_map/ppermute | solution.py:42
  483.5 1.8 collective-permute-start.7
  485.3 38.2 %collective-permute-done.7 = f32[3584,128]{1,0:T(8,128)S(1)} collective-permute-done((f32[3584,128]{1,0:T(8,128)S(1)}, f32[3584,128]{1,0:T(8,128)S(1)}, u32[]{:S(2)}, u32[]{:S(2)}) %collective-permute-start.7) | collective-permute-done | bytes 1835040 | tf_op jit(solution)/shard_map/ppermute | solution.py:42
  523.5 1.4 add.102
  524.9 2.7 collective-permute-start.8
  527.8 0.6 sqrt_reduce_fusion.2
  530.2 0.6 sqrt_reduce_fusion.1
  530.8 73.7 %collective-permute-done.8 = f32[3584,128]{1,0:T(8,128)} collective-permute-done((f32[3584,128]{1,0:T(8,128)}, f32[3584,128]{1,0:T(8,128)}, u32[]{:S(2)}, u32[]{:S(2)}) %collective-permute-start.8) | collective-permute-done | bytes 1835040 | tf_op jit(solution)/shard_map/ppermute | solution.py:42
  604.6 2.3 fusion.2
  606.9 0.9 copy-done.1
  607.8 5.1 convolution_bitcast_fusion.2
  613.6 1.0 copy.12
  616.5 0.6 sqrt_reduce_fusion.5
  617.1 1.7 fusion.10
  618.8 41.7 %all-reduce = (f32[]{:T(128)}, f32[]{:T(128)}, f32[]{:T(128)}, f32[]{:T(128)}, f32[]{:T(128)}, /*index=5*/f32[]{:T(128)}, f32[]{:T(128)}, f32[]{:T(128)}, f32[]{:T(128)}, f32[1]{0:T(128)}, /*index=10*/f32[1]{0:T(128)}) all-reduce(f32[]{:T(128)} %get-tuple-element.12, ...), channel_id=1, replica_groups=mesh['feat'=8,'samp'=4] {'feat','samp'}, use_global_device_ids=true, to_apply=%region_35.0 | all-reduce | flops 11 | bytes 88 | tf_op jit(solution)/shard_map/psum | solution.py:60
  664.3 1.9 pad_maximum_fusion.2
  666.2 1.1 multiply_reduce_fusion.4
  667.3 0.7 sqrt_reduce_fusion.4
  667.9 21.3 %all-reduce.1 = (f32[]{:T(128)}, f32[]{:T(128)}, f32[]{:T(128)}) all-reduce(f32[]{:T(128)} %sqrt_reduce_fusion.4, f32[]{:T(128)} %sqrt_reduce_fusion.5, f32[]{:T(128)} %sqrt_reduce_fusion.6), channel_id=1, replica_groups=mesh['feat'=8,'samp'=4] {'feat'}, use_global_device_ids=true, to_apply=%region_19.0 | all-reduce | flops 3 | bytes 24 | tf_op jit(solution)/shard_map/pmax | solution.py:59
  697.6 0.6 pad_maximum_fusion
  (50 shorter events, 4.7 us)
Async XLA Ops:
  7.2 210.5 %all-reduce.11.cloned.1.call-start = ((), (), s32[]{:S(2)}) async-start(), calls=%async_computation.2 | async-start | bytes 2097152 | tf_op jit(solution)/shard_map/psum | solution.py:56
  7.2 92.8 %slice-start = ((s8[7340032]{0:T(1024)(128)(4,1)}), s8[4194304]{0:T(1024)(128)(4,1)S(1)}, s32[]{:S(2)}) async-start(s8[7340032]{0:T(1024)(128)(4,1)} %bitcast.32), calls=%async_computation.3 | async-start | bytes 8388608
  12.6 87.4 %slice-start.1 = ((s8[7340032]{0:T(1024)(128)(4,1)}), s8[3145728]{0:T(1024)(128)(4,1)S(1)}, s32[]{:S(2)}) async-start(s8[7340032]{0:T(1024)(128)(4,1)} %bitcast.32), calls=%async_computation.4 | async-start | bytes 6291456
  12.6 43.1 %collective-permute-start = (f32[3584,128]{1,0:T(8,128)S(1)}, f32[3584,128]{1,0:T(8,128)S(1)}, u32[]{:S(2)}, u32[]{:S(2)}) collective-permute-start(f32[3584,128]{1,0:T(8,128)S(1)} %fusion.5), channel_id=1, source_target_pairs={{0,4},{4,0},{8,12},{12,8},{16,20},{20,16},{24,28},{28,24},{1,5},{5... | collective-permute-start | bytes 5505032 | tf_op jit(solution)/shard_map/ppermute | solution.py:42
  55.9 44.0 %copy-start = (bf16[3584,128]{1,0:T(8,128)(2,1)S(1)}, bf16[3584,128]{1,0:T(8,128)(2,1)}, u32[]{:S(2)}) copy-start(bf16[3584,128]{1,0:T(8,128)(2,1)} %param.6) | copy-start | bytes 2752516
  55.9 41.2 %collective-permute-start.1 = (f32[3584,128]{1,0:T(8,128)S(1)}, f32[3584,128]{1,0:T(8,128)S(1)}, u32[]{:S(2)}, u32[]{:S(2)}) collective-permute-start(f32[3584,128]{1,0:T(8,128)S(1)} %add.93), channel_id=1, source_target_pairs={{0,8},{4,12},{8,0},{12,4},{16,24},{20,28},{24,16},{28,20},{1,9},{5... | collective-permute-start | bytes 5505032 | tf_op jit(solution)/shard_map/ppermute | solution.py:42
  97.4 80.6 %collective-permute-start.2 = (f32[3584,128]{1,0:T(8,128)S(1)}, f32[3584,128]{1,0:T(8,128)S(1)}, u32[]{:S(2)}, u32[]{:S(2)}) collective-permute-start(f32[3584,128]{1,0:T(8,128)S(1)} %add.94), channel_id=1, source_target_pairs={{0,16},{4,20},{8,24},{12,28},{16,0},{20,4},{24,8},{28,12},{1,17},{... | collective-permute-start | bytes 5505032 | tf_op jit(solution)/shard_map/ppermute | solution.py:42
  180.3 4.7 copy-start.4
  180.3 12.8 %copy-start.6 = (s32[2,1024]{1,0:T(2,128)S(1)}, s32[2,1024]{1,0:T(2,128)}, u32[]{:S(2)}) copy-start(s32[2,1024]{1,0:T(2,128)} %param.8) | copy-start | bytes 24580
  180.3 253.8 %all-reduce.7.cloned.1.call-start = ((), (), s32[]{:S(2)}) async-start(), calls=%async_computation | async-start | bytes 1048576 | tf_op jit(solution)/shard_map/psum | solution.py:56
  249.5 37.5 %collective-permute-start.3 = (f32[3584,128]{1,0:T(8,128)S(1)}, f32[3584,128]{1,0:T(8,128)S(1)}, u32[]{:S(2)}, u32[]{:S(2)}) collective-permute-start(f32[3584,128]{1,0:T(8,128)S(1)} %convolution_bitcast_fusion.1), channel_id=1, source_target_pairs={{0,4},{4,0},{8,12},{12,8},{16,20},{20,16},{24,28},{28,24},{1,5},{5... | collective-permute-start | bytes 5505032 | tf_op jit(solution)/shard_map/ppermute | solution.py:42
  287.0 113.4 %slice-start.2 = ((s8[7340032]{0:T(1024)(128)(4,1)}), s8[4194304]{0:T(1024)(128)(4,1)S(1)}, s32[]{:S(2)}) async-start(s8[7340032]{0:T(1024)(128)(4,1)} %bitcast.34), calls=%async_computation.5 | async-start | bytes 8388608
  287.2 113.2 %slice-start.3 = ((s8[7340032]{0:T(1024)(128)(4,1)}), s8[3145728]{0:T(1024)(128)(4,1)S(1)}, s32[]{:S(2)}) async-start(s8[7340032]{0:T(1024)(128)(4,1)} %bitcast.34), calls=%async_computation.6 | async-start | bytes 6291456
  287.2 37.8 %collective-permute-start.4 = (f32[3584,128]{1,0:T(8,128)S(1)}, f32[3584,128]{1,0:T(8,128)S(1)}, u32[]{:S(2)}, u32[]{:S(2)}) collective-permute-start(f32[3584,128]{1,0:T(8,128)S(1)} %add.97), channel_id=1, source_target_pairs={{0,8},{4,12},{8,0},{12,4},{16,24},{20,28},{24,16},{28,20},{1,9},{5... | collective-permute-start | bytes 5505032 | tf_op jit(solution)/shard_map/ppermute | solution.py:42
  325.2 74.9 %collective-permute-start.5 = (f32[3584,128]{1,0:T(8,128)S(1)}, f32[3584,128]{1,0:T(8,128)S(1)}, u32[]{:S(2)}, u32[]{:S(2)}) collective-permute-start(f32[3584,128]{1,0:T(8,128)S(1)} %add.98), channel_id=1, source_target_pairs={{0,16},{4,20},{8,24},{12,28},{16,0},{20,4},{24,8},{28,12},{1,17},{... | collective-permute-start | bytes 5505032 | tf_op jit(solution)/shard_map/ppermute | solution.py:42
  402.4 263.8 %all-reduce.9.cloned.1.call-start = ((), (), s32[]{:S(2)}) async-start(), calls=%async_computation.1 | async-start | bytes 1048576 | tf_op jit(solution)/shard_map/psum | solution.py:56
  437.2 5.5 copy-start.2
  442.6 40.6 %collective-permute-start.6 = (f32[3584,128]{1,0:T(8,128)S(1)}, f32[3584,128]{1,0:T(8,128)S(1)}, u32[]{:S(2)}, u32[]{:S(2)}) collective-permute-start(f32[3584,128]{1,0:T(8,128)S(1)} %convolution_bitcast_fusion), channel_id=1, source_target_pairs={{0,4},{4,0},{8,12},{12,8},{16,20},{20,16},{24,28},{28,24},{1,5},{5... | collective-permute-start | bytes 5505032 | tf_op jit(solution)/shard_map/ppermute | solution.py:42
  483.5 44.1 %copy-start.5 = (f32[1024,128]{1,0:T(8,128)S(1)}, f32[1024,128]{1,0:T(8,128)}, u32[]{:S(2)}) copy-start(f32[1024,128]{1,0:T(8,128)} %param.7) | copy-start | bytes 1572868
  483.5 40.0 %collective-permute-start.7 = (f32[3584,128]{1,0:T(8,128)S(1)}, f32[3584,128]{1,0:T(8,128)S(1)}, u32[]{:S(2)}, u32[]{:S(2)}) collective-permute-start(f32[3584,128]{1,0:T(8,128)S(1)} %add.101), channel_id=1, source_target_pairs={{0,8},{4,12},{8,0},{12,4},{16,24},{20,28},{24,16},{28,20},{1,9},{5... | collective-permute-start | bytes 5505032 | tf_op jit(solution)/shard_map/ppermute | solution.py:42
  524.9 79.7 %collective-permute-start.8 = (f32[3584,128]{1,0:T(8,128)}, f32[3584,128]{1,0:T(8,128)}, u32[]{:S(2)}, u32[]{:S(2)}) collective-permute-start(f32[3584,128]{1,0:T(8,128)} %add.102), channel_id=1, source_target_pairs={{0,16},{4,20},{8,24},{12,28},{16,0},{20,4},{24,8},{28,12},{1,17},{... | collective-permute-start | bytes 5505032 | tf_op jit(solution)/shard_map/ppermute | solution.py:42
  606.9 0.9 copy-start.1
  607.8 5.8 copy-start.3
Sparse Core Ops, SparseCore 0:
  180.4 37.1 all-reduce.10
  402.5 31.5 all-reduce.6
  613.1 34.9 all-reduce.8
